TPU v7x, 32 devices: a whole 2x2x4 slice. The times are simulated.
32 devices in a mesh: gx: 8 (over z, x), gy: 4 (over y, core).
Axes of the slice: x: 2, y: 2, z: 4, core: 2. Of those that a mesh axis runs over, the one named last changes fastest.
Arguments:
- velocity: float32 [3, 8192, 512], P(None, ('gx', 'gy')), may hold values from -6 to 6
- positions: float32 [3, 1024, 256], P(None, ('gx', 'gy')), may hold values from -6 to 6
- stiff_h: float32 [1024, 256], P(('gx', 'gy')), may hold values from 0.1 to 1
- stiff_v: float32 [1024, 256], P(('gx', 'gy')), may hold values from 0.1 to 1
- marker_owner: int32 [262144, 1], P(('gx', 'gy')), may hold values from 0 to 31; in each aligned block of 8192 rows (0 to 8191, 8192 to 16383, ...) at most 384 rows name the same one
- marker_element: int32 [262144], P(('gx', 'gy')), may hold values from 0 to 255
- marker_coords: float32 [3, 262144], P(None, ('gx', 'gy')), may hold values from -1 to 1
Outputs:
- new_positions: float32 [3, 1024, 256], P(None, ('gx', 'gy'))
- node_forces: float32 [3, 8192, 512], P(None, ('gx', 'gy'))
Inputs may be any that keep to these rules, and one draw needn't show every extreme that they name: `marker_owner`: among the markers of one device's rows, no owner is named more than 384 times, and in some devices' rows one owner is named exactly 384 times.
All inputs are finite; a program needn't handle non-finite values.
Results may differ from a plain program's by a relative error of at most 0.00013.
Values sent between devices are 32-bit elements; how exact they have to be, the bound alone decides.
No kernel may reach another device: no remote copies, remote signals or barrier semaphores. Data moves between devices by JAX's collectives and lax.ppermute only.
A program may use at most 64 MiB of HBM per device.

v0:
```python
import math
import jax
import jax.numpy as jnp
from jax import lax
from jax.sharding import PartitionSpec as P

POINTS = 8
bend_modulus = 0.05
time_step = 0.5


def padded(cells, sides, width):
    for axis, dim in sides:
        count = lax.axis_size(axis)
        head = lax.slice_in_dim(cells, 0, width, axis=dim)
        tail = lax.slice_in_dim(cells, cells.shape[dim] - width, cells.shape[dim], axis=dim)
        cells = jnp.concatenate(
            [
                lax.ppermute(tail, axis, [(i, (i + 1) % count) for i in range(count)]),
                cells,
                lax.ppermute(head, axis, [((i + 1) % count, i) for i in range(count)]),
            ],
            axis=dim,
        )
    return cells


def basis(values):
    abscissa = -jnp.cos(jnp.pi * jnp.arange(POINTS).astype(values.dtype) / (POINTS - 1))
    collected = []
    for i in range(POINTS):
        product = jnp.ones_like(values)
        for j in range(POINTS):
            if j != i:
                product = product * ((values - abscissa[j]) / (abscissa[i] - abscissa[j]))
        collected.append(product)
    return jnp.stack(collected)


def weight_table(factors):
    along_r = factors[0:POINTS].T
    along_s = factors[POINTS : 2 * POINTS].T
    along_t = factors[2 * POINTS : 3 * POINTS].T
    table = along_r[:, :, None, None] * along_s[:, None, :, None] * along_t[:, None, None, :]
    return table.reshape(along_r.shape[0], POINTS * POINTS * POINTS)


def surface_laplacian(extended):
    middle = extended[:, 1:-1]
    return (
        extended[:, 2:]
        + extended[:, :-2]
        + jnp.roll(middle, 1, axis=2)
        + jnp.roll(middle, -1, axis=2)
        - 4.0 * middle
    )


def tension(extended, stiff_h):
    points = extended[:3]
    vertical = extended[3]
    middle = points[:, 1:-1]
    return (
        stiff_h * (jnp.roll(middle, -1, axis=2) - middle)
        + jnp.roll(stiff_h, 1, axis=1) * (jnp.roll(middle, 1, axis=2) - middle)
        + vertical[1:-1] * (points[:, 2:] - middle)
        + vertical[:-2] * (points[:, :-2] - middle)
    )


def three_factors(coords):
    return jnp.concatenate([basis(coords[0]), basis(coords[1]), basis(coords[2])], axis=0)


def selector_of(block_elements, elem_count):
    return (block_elements[:, None] == jnp.arange(elem_count, dtype=jnp.int32)[None, :]).astype(
        jnp.float32
    )


def local(velocity, positions, stiff_h, stiff_v, marker_owner, marker_element, marker_coords):
    major_count = lax.axis_size("gx")
    minor_count = lax.axis_size("gy")
    devices_all = major_count * minor_count
    marker_count = marker_owner.shape[0]
    capacity = 3 * marker_count // (2 * devices_all)
    slot_total = devices_all * capacity
    elem_count = velocity.shape[1]
    stacked = jnp.concatenate([positions, stiff_v[None]], axis=0)
    extended = padded(stacked, ((("gx", "gy"), 1),), 1)
    pulling = tension(extended, stiff_h)
    laplace = surface_laplacian(extended[:3])
    laplace_wide = padded(laplace, ((("gx", "gy"), 1),), 1)
    bending = -bend_modulus * surface_laplacian(laplace_wide)
    marker_force = (pulling + bending).reshape(3, marker_count)
    owners = marker_owner[:, 0]
    ordering = jnp.argsort(owners, stable=True)
    sorted_owners = owners[ordering]
    offsets = jnp.searchsorted(sorted_owners, jnp.arange(devices_all, dtype=jnp.int32), side="left")
    within = jnp.arange(marker_count, dtype=jnp.int32) - offsets[sorted_owners]
    places = (
        jnp.zeros((marker_count,), jnp.int32).at[ordering].set(sorted_owners * capacity + within)
    )
    described = three_factors(marker_coords)
    lead = described.shape[0]
    payload = jnp.concatenate([described, marker_force], axis=0)
    width_all = payload.shape[0]
    outgoing = jnp.zeros((width_all, slot_total), jnp.float32).at[:, places].set(payload)
    slot_ids = jnp.zeros((1, slot_total), jnp.int32).at[:, places].set(marker_element[None])
    got_floats, got_slots = (
        lax.all_to_all(
            lax.all_to_all(
                outgoing.reshape(width_all, major_count, minor_count, capacity),
                "gx",
                split_axis=1,
                concat_axis=1,
                tiled=True,
            ),
            "gy",
            split_axis=2,
            concat_axis=2,
            tiled=True,
        ),
        lax.all_to_all(
            lax.all_to_all(
                slot_ids.reshape(1, major_count, minor_count, capacity),
                "gx",
                split_axis=1,
                concat_axis=1,
                tiled=True,
            ),
            "gy",
            split_axis=2,
            concat_axis=2,
            tiled=True,
        ),
    )
    got_floats = got_floats.reshape(width_all, slot_total)
    element_ids = got_slots.reshape(slot_total)
    factors = got_floats[:lead]
    pushes = got_floats[lead:]
    block_len = math.gcd(slot_total, 512)
    block_count = slot_total // block_len
    factor_blocks = factors.reshape(3 * POINTS, block_count, block_len).transpose(1, 0, 2)
    element_blocks = element_ids.reshape(block_count, block_len)
    push_blocks = pushes.reshape(3, block_count, block_len).transpose(1, 0, 2)

    def sample(inputs):
        block_factors, block_elements = inputs
        weights = weight_table(block_factors)
        selector = selector_of(block_elements, elem_count)
        gathered = jnp.einsum("be,ken->kbn", selector, velocity, precision=lax.Precision.HIGHEST)
        return jnp.sum(gathered * weights[None], axis=-1)

    sampled = lax.map(sample, (factor_blocks, element_blocks))
    returning = sampled.transpose(1, 0, 2).reshape(3, slot_total)
    arrived = lax.all_to_all(
        lax.all_to_all(
            returning.reshape(3, major_count, minor_count, capacity),
            "gx",
            split_axis=1,
            concat_axis=1,
            tiled=True,
        ),
        "gy",
        split_axis=2,
        concat_axis=2,
        tiled=True,
    )

    def deposit(running, inputs):
        block_factors, block_elements, block_pushes = inputs
        weights = weight_table(block_factors)
        selector = selector_of(block_elements, elem_count)
        loads = block_pushes[:, :, None] * weights[None]
        added = jnp.einsum("be,kbn->ken", selector, loads, precision=lax.Precision.HIGHEST)
        return (running + added, None)

    node_forces, unused = lax.scan(
        deposit, jnp.zeros_like(velocity), (factor_blocks, element_blocks, push_blocks)
    )
    moved = jnp.take(arrived.reshape(3, slot_total), places, axis=1).reshape(positions.shape)
    return (positions + time_step * moved, node_forces)


def solution(mesh):
    return jax.shard_map(
        local,
        mesh=mesh,
        in_specs=(
            P(None, ("gx", "gy"), None),
            P(None, ("gx", "gy"), None),
            P(("gx", "gy"), None),
            P(("gx", "gy"), None),
            P(("gx", "gy"), None),
            P(("gx", "gy")),
            P(None, ("gx", "gy")),
        ),
        out_specs=(P(None, ("gx", "gy"), None), P(None, ("gx", "gy"), None)),
        check_vma=False,
    )
```

profile of v0, /device:TPU:0, one launch (start us, length us, event | category | flops | bytes accessed | tf_op | source)
XLA Modules:
  0.0 586.4 jit_solution(10198000036078593590)
XLA Ops:
  2.0 6.0 %collective-permute-start = (f32[4,1,256]{2,1,0:T(1,128)S(1)}, f32[4,1,256]{2,1,0:T(1,128)S(1)}, u32[]{:S(2)}, u32[]{:S(2)}) collective-permute-start(f32[4,1,256]{2,1,0:T(1,128)S(1)} %get-tuple-element.267), channel_id=1, source_target_pairs={{1,0},{2,1},{3,2},{4,3},{5,4},{6,5},{7,6},{8,7},{9,8},{10,9},{11,1... | collective-permute-start | bytes 12296 | tf_op jit(solution)/shard_map/ppermute | solution.py:21
  8.0 7.5 %sort.17 = (s32[8192]{0:T(1024)}, s32[8192]{0:T(1024)S(1)}) sort(s32[8192]{0:T(1024)} %bitcast.127, s32[8192]{0:T(1024)S(1)} %iota.23), dimensions={0}, to_apply=%region_0.1 | sort | flops 106496 | bytes 131072 | tf_op jit(solution)/shard_map/jit(argsort)/sort | solution.py:97
  15.5 45.5 %gather_fusion.1 = s32[8192]{0:T(1024)S(1)} fusion(s32[8192]{0:T(1024)S(1)} %bitcast.128, s32[8192]{0:T(1024)S(1)} %get-tuple-element.305), kind=kCustom, calls=%fused_computation.1 | custom fusion | bytes 98304 | tf_op jit(solution)/shard_map/gather | solution.py:98
  61.1 10.5 %while.46 = (s32[]{:T(128)}, u32[32]{0:T(128)S(1)}, u32[32]{0:T(128)S(1)}, s32[8192]{0:T(1024)S(1)}, s32[]{:T(128)}, /*index=5*/s32[]{:T(128)}, s32[]{}) while((s32[]{:T(128)}, u32[32]{0:T(128)S(1)}, u32[32]{0:T(128)S(1)}, s32[8192]{0:T(1024)S(1)}, s32[]{:T(128)}, /*index=5*/s32[]{:T(128)}, s32[]{}) %tuple.172), condition=%wide.region_2.3_spmd.clone, body=%wide.region_1.2_spmd.clone.sunk | while | flops 1444 | bytes 5732 | solution.py:99
  80.0 15.9 %fusion.35 = s32[8192]{0:T(1024)S(1)} fusion(pred[8192]{0:T(1024)(128)(4,1)S(1)} %get-tuple-element.228, pred[8192]{0:T(1024)(128)(4,1)S(1)} %get-tuple-element.227, pred[8192]{0:T(1024)(128)(4,1)S(1)} %get-tuple-element.226, pred[8192]{0:T(1024)(128)(4,1)S(1)} %get-tuple-element.225, pred[8192]{0:T(1024)(128)(4,1)S(1)} %get-tuple-element.224, ...), kind=kLoop, calls=%fused_computation.250 | loop fusion | flops 229376 | bytes 303204 | tf_op jit(solution)/shard_map/add | solution.py:102
  95.9 30.5 %scatter_custom_fusion = s32[8192]{0:T(1024)S(1)} fusion(s32[8192]{0:T(1024)S(1)} %get-tuple-element.306, s32[8192]{0:T(1024)S(1)} %fusion.35, s32[]{:T(128)} %constant.79.clone.1), kind=kCustom, calls=%fused_computation.280 | custom fusion | bytes 32772 | tf_op jit(solution)/shard_map/scatter | solution.py:102
  126.4 30.7 %scatter_custom_fusion.1 = s32[12288]{0:T(1024)S(1)} fusion(s32[8192]{0:T(1024)S(1)} %get-tuple-element.304, s32[8192]{0:T(1024)} %param.18, s32[]{:T(128)} %constant.79.clone.1), kind=kCustom, calls=%fused_computation.252 | custom fusion | bytes 49664 | tf_op jit(solution)/shard_map/scatter | solution.py:109
  231.5 4.8 divide_multiply_fusion
  236.3 4.9 divide_multiply_fusion.6
  241.2 4.9 divide_multiply_fusion.12
  246.1 4.9 divide_multiply_fusion.18
  250.9 4.9 divide_multiply_fusion.24
  255.8 4.9 divide_multiply_fusion.30
  260.7 4.8 divide_multiply_fusion.36
  265.5 4.9 divide_multiply_fusion.42
  274.9 5.3 collective-permute-done.3
  284.4 23.9 %scatter_custom_fusion.2 = f32[27,12288]{0,1:T(8,128)} fusion(s32[8192]{0:T(1024)S(1)} %get-tuple-element.304, f32[8192,27]{1,0:T(8,128)} %copy.89, f32[]{:T(128)} %constant.87.clone.1), kind=kCustom, calls=%fused_computation.41 | custom fusion | bytes 1327616 | tf_op jit(solution)/shard_map/scatter | solution.py:108
  308.2 5.5 copy.90
  318.0 26.6 %all-to-all-done.2 = f32[27,8,4,384]{3,2,0,1:T(4,128)S(1)} async-done(((f32[27,8,4,384]{3,2,0,1:T(4,128)}), f32[27,8,4,384]{3,2,0,1:T(4,128)S(1)}, u32[]{:S(2)}, u32[]{:S(2)}) %all-to-all-start.2) | async-done | bytes 1327136 | tf_op jit(solution)/shard_map/all_to_all | solution.py:112
  357.5 16.7 %all-to-all-done.3 = f32[27,8,4,384]{3,1,0,2:T(8,128)} async-done(((f32[27,8,4,384]{3,1,0,2:T(8,128)}), f32[27,8,4,384]{3,1,0,2:T(8,128)}, u32[]{:S(2)}, u32[]{:S(2)}) %all-to-all-start.3) | async-done | bytes 1327136 | tf_op jit(solution)/shard_map/all_to_all | solution.py:111
  380.9 64.9 %while.45 = (s32[]{:T(128)}, f32[24,3,512]{2,1,0:T(4,128)S(1)}, s32[24,512]{1,0:T(8,128)S(1)}, f32[3,256,512]{1,2,0:T(8,128)S(1)}, f32[24,24,512]{2,1,0:T(8,128)}, /*index=5*/s32[]{:T(128)}, s32[]{:T(128)}, s32[]{}, s32[]{}) while((s32[]{:T(128)}, f32[24,3,512]{2,1,0:T(4,128)S(1)}, s32[24,512]{1,0:T(8,128)S(1)}, f32[3,256,512]{1,2,0:T(8,128)S(1)}, ...), condition=%wide.region_8.9_spmd, body=%wide.region_6.8_spmd.sunk | while | flops 2417916416 | bytes 4108425 | solution.py:155
  451.5 6.4 %all-to-all-done.4 = f32[3,8,4,384]{3,2,0,1:T(4,128)S(1)} async-done(((f32[3,8,4,384]{3,2,0,1:T(4,128)}), f32[3,8,4,384]{3,2,0,1:T(4,128)S(1)}, u32[]{:S(2)}, u32[]{:S(2)}) %all-to-all-start.4) | async-done | bytes 147488 | tf_op jit(solution)/shard_map/all_to_all | solution.py:158
  461.8 85.0 %while.47 = (s32[]{:T(128)}, f32[3,256,512]{1,2,0:T(8,128)S(1)}, f32[24,3,512]{2,0,1:T(8,128)S(1)}, f32[24,24,512]{2,1,0:T(8,128)}, s32[24,512]{1,0:T(8,128)S(1)}, /*index=5*/s32[]{:T(128)}, s32[]{:T(128)}, s32[]{}, s32[]{}) while((s32[]{:T(128)}, f32[3,256,512]{1,2,0:T(8,128)S(1)}, f32[24,3,512]{2,0,1:T(8,128)S(1)}, ...), condition=%wide.region_10.11_spmd.clone, body=%wide.region_9.10_spmd.clone.sunk | while | flops 2417917952 | bytes 5689491 | solution.py:179
  552.4 30.5 %gather_fusion.2 = f32[8192,3]{1,0:T(8,128)} fusion(f32[3,12288]{0,1:T(8,128)} %bitcast.133, s32[8192]{0:T(1024)S(1)} %get-tuple-element.303), kind=kCustom, calls=%fused_computation.2 | custom fusion | bytes 229376 | tf_op jit(solution)/shard_map/jit(_take)/gather | solution.py:182
  (446 shorter events, 223.5 us)
Async XLA Ops:
  0.6 14.9 %copy-start = (s32[8192,1]{0,1:T(1,128)S(1)}, s32[8192,1]{0,1:T(1,128)}, u32[]{:S(2)}) copy-start(s32[8192,1]{0,1:T(1,128)} %param.17) | copy-start | bytes 98308
  1.4 269.1 %collective-permute-start.1 = (f32[4,1,256]{2,1,0:T(1,128)S(1)}, f32[4,1,256]{2,1,0:T(1,128)S(1)}, u32[]{:S(2)}, u32[]{:S(2)}) collective-permute-start(f32[4,1,256]{2,1,0:T(1,128)S(1)} %get-tuple-element.268), channel_id=1, source_target_pairs={{0,1},{1,2},{2,3},{3,4},{4,5},{5,6},{6,7},{7,8},{8,9},{9,10},{10,1... | collective-permute-start | bytes 12296 | tf_op jit(solution)/shard_map/ppermute | solution.py:19
  2.0 268.6 %collective-permute-start = (f32[4,1,256]{2,1,0:T(1,128)S(1)}, f32[4,1,256]{2,1,0:T(1,128)S(1)}, u32[]{:S(2)}, u32[]{:S(2)}) collective-permute-start(f32[4,1,256]{2,1,0:T(1,128)S(1)} %get-tuple-element.267), channel_id=1, source_target_pairs={{1,0},{2,1},{3,2},{4,3},{5,4},{6,5},{7,6},{8,7},{9,8},{10,9},{11,1... | collective-permute-start | bytes 12296 | tf_op jit(solution)/shard_map/ppermute | solution.py:21
  61.0 170.1 %copy-start.1 = (f32[3,32,256]{2,1,0:T(8,128)S(1)}, f32[3,32,256]{2,1,0:T(8,128)}, u32[]{:S(2)}) copy-start(f32[3,32,256]{2,1,0:T(8,128)} %param.14) | copy-start | bytes 294916
  71.6 159.8 %copy-start.5 = (f32[32,256]{1,0:T(8,128)S(1)}, f32[32,256]{1,0:T(8,128)}, u32[]{:S(2)}) copy-start(f32[32,256]{1,0:T(8,128)} %param.15) | copy-start | bytes 98308
  71.6 159.8 %copy-start.2 = (f32[3,8192]{1,0:T(4,128)S(1)}, f32[3,8192]{1,0:T(4,128)}, u32[]{:S(2)}) copy-start(f32[3,8192]{1,0:T(4,128)} %param.19) | copy-start | bytes 294916
  80.0 190.5 %copy-start.4 = (f32[32,256]{1,0:T(8,128)S(1)}, f32[32,256]{1,0:T(8,128)}, u32[]{:S(2)}) copy-start(f32[32,256]{1,0:T(8,128)} %param.16) | copy-start | bytes 98308
  157.8 156.0 %all-to-all-start = ((s32[1,8,4,384]{3,2,0,1:T(4,128)}), s32[1,8,4,384]{3,2,0,1:T(4,128)S(1)}, u32[]{:S(2)}, u32[]{:S(2)}) async-start(s32[1,8,4,384]{3,2,0,1:T(4,128)} %reshape.123), calls=%async_computation | async-start | bytes 98304 | tf_op jit(solution)/shard_map/all_to_all | solution.py:125
  270.9 4.0 collective-permute-start.2
  273.5 6.6 %collective-permute-start.3 = (f32[3,1,256]{2,1,0:T(1,128)S(1)}, f32[3,1,256]{2,1,0:T(1,128)S(1)}, u32[]{:S(2)}, u32[]{:S(2)}) collective-permute-start(f32[3,1,256]{2,1,0:T(1,128)S(1)} %get-tuple-element.298), channel_id=1, source_target_pairs={{0,1},{1,2},{2,3},{3,4},{4,5},{5,6},{6,7},{7,8},{8,9},{9,10},{10,1... | collective-permute-start | bytes 9224 | tf_op jit(solution)/shard_map/ppermute | solution.py:19
  313.8 30.8 %all-to-all-start.2 = ((f32[27,8,4,384]{3,2,0,1:T(4,128)}), f32[27,8,4,384]{3,2,0,1:T(4,128)S(1)}, u32[]{:S(2)}, u32[]{:S(2)}) async-start(f32[27,8,4,384]{3,2,0,1:T(4,128)} %copy.90), calls=%async_computation.2 | async-start | bytes 2654208 | tf_op jit(solution)/shard_map/all_to_all | solution.py:112
  344.6 7.8 %all-to-all-start.1 = ((s32[1,8,4,384]{3,1,0,2:T(8,128)}), s32[1,8,4,384]{3,1,0,2:T(8,128)S(1)}, u32[]{:S(2)}, u32[]{:S(2)}) async-start(s32[1,8,4,384]{3,1,0,2:T(8,128)} %copy.87), calls=%async_computation.1 | async-start | bytes 98304 | tf_op jit(solution)/shard_map/all_to_all | solution.py:124
  349.5 7.4 %copy-start.3 = (f32[3,256,512]{2,1,0:T(8,128)S(1)}, f32[3,256,512]{2,1,0:T(8,128)}, u32[]{:S(2)}) copy-start(f32[3,256,512]{2,1,0:T(8,128)} %param.13) | copy-start | bytes 4718596
  352.4 21.8 %all-to-all-start.3 = ((f32[27,8,4,384]{3,1,0,2:T(8,128)}), f32[27,8,4,384]{3,1,0,2:T(8,128)}, u32[]{:S(2)}, u32[]{:S(2)}) async-start(f32[27,8,4,384]{3,1,0,2:T(8,128)} %copy.91), calls=%async_computation.3 | async-start | bytes 2654208 | tf_op jit(solution)/shard_map/all_to_all | solution.py:111
  446.6 11.2 %all-to-all-start.4 = ((f32[3,8,4,384]{3,2,0,1:T(4,128)}), f32[3,8,4,384]{3,2,0,1:T(4,128)S(1)}, u32[]{:S(2)}, u32[]{:S(2)}) async-start(f32[3,8,4,384]{3,2,0,1:T(4,128)} %copy.96), calls=%async_computation.4 | async-start | bytes 294912 | tf_op jit(solution)/shard_map/all_to_all | solution.py:158
  458.5 90.0 %all-to-all-start.5 = ((f32[3,8,4,384]{3,1,0,2:T(8,128)}), f32[3,8,4,384]{3,1,0,2:T(8,128)S(1)}, u32[]{:S(2)}, u32[]{:S(2)}) async-start(f32[3,8,4,384]{3,1,0,2:T(8,128)} %copy.97), calls=%async_computation.5 | async-start | bytes 294912 | tf_op jit(solution)/shard_map/all_to_all | solution.py:157
where the time goes:
time: 596 us; the launch traced here: 586 us
  local copies, waits for them, and re-layouts  242 us (41%)
  matrix products  103 us (17%)
  other arithmetic  78.1 us (13%)
  between operations  70.2 us (12%)
  waiting for transfers between devices  59.2 us (10%)
  starting transfers between devices  31.7 us (5%)
    dot_general x24, matrix products, deposit(): jnp.einsum('be,kbn->ken', selector, loads, precision=lax.Precision.HIGHEST)  60.9 us
    gather x1, local copies, waits for them, and re-layouts, local(): sorted_owners = owners[ordering]  45.5 us
    dot_general x24, matrix products, sample(): jnp.einsum('be,ken->kbn', selector, velocity, precision=lax.Precision.HIG...  41.8 us
    mul x8, other arithmetic, basis(): product = product * ((values - abscissa[j]) / (abscissa[i] - abscissa[j]))  39 us
    transpose x48, local copies, waits for them, and re-layouts, weight_table(): along_r = factors[0:POINTS].T  36.7 us
    gather x2, local copies, waits for them, and re-layouts, local(): jnp.take(arrived.reshape(3, slot_total), places, axis=1)  33.3 us
    scatter x1, local copies, waits for them, and re-layouts, local(): jnp.zeros((1, slot_total), jnp.int32).at[:, places]  30.7 us
    scatter x1, local copies, waits for them, and re-layouts, local(): jnp.zeros((marker_count,), jnp.int32).at[ordering]  30.5 us
  transfers between devices with their start and end apart: 10, of which 6 were waited for; matrix products, arithmetic and copies ran while one was open for 53% of the time, Pallas kernels for 0%

commit v1 on v0

--- a/solution.py
+++ b/solution.py
@@ -7,6 +7,29 @@
 POINTS = 8
 bend_modulus = 0.05
 time_step = 0.5
+
+
+def in_blocks(array, dim, length):
+    shape = array.shape
+    tiles = array.reshape(*shape[:dim], length, shape[dim] // length, *shape[dim + 1 :])
+    return jnp.moveaxis(tiles, dim, 0)
+
+
+def laid_out(blocks, dim):
+    lengths = list(blocks.shape[1:])
+    lengths[dim] *= blocks.shape[0]
+    return jnp.moveaxis(blocks, 0, dim).reshape(lengths)
+
+
+def pairwise_exchange(x, axis, split_dim, concat_dim):
+    size, position = (lax.axis_size(axis), lax.axis_index(axis))
+    tiles = in_blocks(x, split_dim, size)
+    outs = [tiles[position]]
+    for step in range(1, size):
+        sent = tiles[position ^ step]
+        outs.append(lax.ppermute(sent, axis, [(i, i ^ step) for i in range(size)]))
+    tiles = jnp.stack(outs)[position ^ jnp.arange(size)]
+    return laid_out(tiles, concat_dim)
 
 
 def padded(cells, sides, width):
@@ -109,12 +132,8 @@
     slot_ids = jnp.zeros((1, slot_total), jnp.int32).at[:, places].set(marker_element[None])
     got_floats, got_slots = (
         lax.all_to_all(
-            lax.all_to_all(
-                outgoing.reshape(width_all, major_count, minor_count, capacity),
-                "gx",
-                split_axis=1,
-                concat_axis=1,
-                tiled=True,
+            pairwise_exchange(
+                outgoing.reshape(width_all, major_count, minor_count, capacity), "gx", 1, 1
             ),
             "gy",
             split_axis=2,

time: 596 us -> 599 us (level)
  waiting for transfers between devices: 59.2 us -> 34.3 us
  local copies, waits for them, and re-layouts: 242 us -> 258 us
  starting transfers between devices: 31.7 us -> 43.4 us
    all_to_all x2 -> x1, waiting for transfers between devices: 43.3 us -> 16.9 us  [local(): lax.all_to_all(pairwise_exchange(outgoing.reshape(width_all, major_count,...]
    another operation x0 -> x10, local copies, waits for them, and re-layouts: none -> 15.5 us
    ppermute x0 -> x7, starting transfers between devices: none -> 11.2 us  [pairwise_exchange(): outs.append(lax.ppermute(sent, axis, [(i, i ^ step) for i in range(size)]))]
  transfers between devices with their start and end apart: 10 -> 16, of which waited for: 6 -> 5; matrix products, arithmetic and copies ran while one was open for 53% -> 56% of each run, Pallas kernels for 0% -> 0%
where the time goes in v1:
time: 599 us; the launch traced here: 589 us
  local copies, waits for them, and re-layouts  258 us (43%)
  matrix products  103 us (17%)
  other arithmetic  78.1 us (13%)
  between operations  70.4 us (12%)
  starting transfers between devices  43.4 us (7%)
  waiting for transfers between devices  34.3 us (6%)
    dot_general x24, matrix products, deposit(): jnp.einsum('be,kbn->ken', selector, loads, precision=lax.Precision.HIGHEST)  60.9 us
    gather x1, local copies, waits for them, and re-layouts, local(): sorted_owners = owners[ordering]  45.5 us
    dot_general x24, matrix products, sample(): jnp.einsum('be,ken->kbn', selector, velocity, precision=lax.Precision.HIG...  41.8 us
    mul x8, other arithmetic, basis(): product = product * ((values - abscissa[j]) / (abscissa[i] - abscissa[j]))  39 us
    transpose x48, local copies, waits for them, and re-layouts, weight_table(): along_r = factors[0:POINTS].T  36.7 us
    gather x2, local copies, waits for them, and re-layouts, local(): jnp.take(arrived.reshape(3, slot_total), places, axis=1)  33.3 us
    scatter x1, local copies, waits for them, and re-layouts, local(): jnp.zeros((1, slot_total), jnp.int32).at[:, places]  30.7 us
    scatter x1, local copies, waits for them, and re-layouts, local(): jnp.zeros((marker_count,), jnp.int32).at[ordering]  30.5 us
  transfers between devices with their start and end apart: 16, of which 5 were waited for; matrix products, arithmetic and copies ran while one was open for 56% of the time, Pallas kernels for 0%

profile of v1, /device:TPU:0, one launch (start us, length us, event | category | flops | bytes accessed | tf_op | source)
XLA Modules:
  0.0 589.4 jit_solution(9434356705646395022)
XLA Ops:
  2.0 6.0 %collective-permute-start = (f32[4,1,256]{2,1,0:T(1,128)S(1)}, f32[4,1,256]{2,1,0:T(1,128)S(1)}, u32[]{:S(2)}, u32[]{:S(2)}) collective-permute-start(f32[4,1,256]{2,1,0:T(1,128)S(1)} %get-tuple-element.299), channel_id=1, source_target_pairs={{1,0},{2,1},{3,2},{4,3},{5,4},{6,5},{7,6},{8,7},{9,8},{10,9},{11,1... | collective-permute-start | bytes 12296 | tf_op jit(solution)/shard_map/ppermute | solution.py:44
  8.0 7.5 %sort.17 = (s32[8192]{0:T(1024)}, s32[8192]{0:T(1024)S(1)}) sort(s32[8192]{0:T(1024)} %bitcast.158, s32[8192]{0:T(1024)S(1)} %iota.27), dimensions={0}, to_apply=%region_0.1 | sort | flops 106496 | bytes 131072 | tf_op jit(solution)/shard_map/jit(argsort)/sort | solution.py:120
  15.5 45.5 %gather_fusion.1 = s32[8192]{0:T(1024)S(1)} fusion(s32[8192]{0:T(1024)S(1)} %bitcast.159, s32[8192]{0:T(1024)S(1)} %get-tuple-element.337), kind=kCustom, calls=%fused_computation.1 | custom fusion | bytes 98304 | tf_op jit(solution)/shard_map/gather | solution.py:121
  61.1 10.5 %while.46 = (s32[]{:T(128)}, u32[32]{0:T(128)S(1)}, u32[32]{0:T(128)S(1)}, s32[8192]{0:T(1024)S(1)}, s32[]{:T(128)}, /*index=5*/s32[]{:T(128)}, s32[]{}) while((s32[]{:T(128)}, u32[32]{0:T(128)S(1)}, u32[32]{0:T(128)S(1)}, s32[8192]{0:T(1024)S(1)}, s32[]{:T(128)}, /*index=5*/s32[]{:T(128)}, s32[]{}) %tuple.185), condition=%wide.region_2.3_spmd.clone, body=%wide.region_1.2_spmd.clone.sunk | while | flops 1444 | bytes 5732 | solution.py:122
  80.0 15.9 %fusion.35 = s32[8192]{0:T(1024)S(1)} fusion(pred[8192]{0:T(1024)(128)(4,1)S(1)} %get-tuple-element.252, pred[8192]{0:T(1024)(128)(4,1)S(1)} %get-tuple-element.251, pred[8192]{0:T(1024)(128)(4,1)S(1)} %get-tuple-element.250, pred[8192]{0:T(1024)(128)(4,1)S(1)} %get-tuple-element.249, pred[8192]{0:T(1024)(128)(4,1)S(1)} %get-tuple-element.248, ...), kind=kLoop, calls=%fused_computation.259 | loop fusion | flops 229376 | bytes 303204 | tf_op jit(solution)/shard_map/add | solution.py:125
  95.9 30.5 %scatter_custom_fusion = s32[8192]{0:T(1024)S(1)} fusion(s32[8192]{0:T(1024)S(1)} %get-tuple-element.338, s32[8192]{0:T(1024)S(1)} %fusion.35, s32[]{:T(128)} %constant.60.clone.1), kind=kCustom, calls=%fused_computation.289 | custom fusion | bytes 32772 | tf_op jit(solution)/shard_map/scatter | solution.py:125
  126.4 30.7 %scatter_custom_fusion.1 = s32[12288]{0:T(1024)S(1)} fusion(s32[8192]{0:T(1024)S(1)} %get-tuple-element.336, s32[8192]{0:T(1024)} %param.18, s32[]{:T(128)} %constant.60.clone.1), kind=kCustom, calls=%fused_computation.261 | custom fusion | bytes 49664 | tf_op jit(solution)/shard_map/scatter | solution.py:132
  231.5 4.8 divide_multiply_fusion
  236.4 4.9 divide_multiply_fusion.6
  241.3 4.9 divide_multiply_fusion.12
  246.1 4.9 divide_multiply_fusion.18
  251.0 4.9 divide_multiply_fusion.24
  255.9 4.9 divide_multiply_fusion.30
  260.8 4.8 divide_multiply_fusion.36
  265.6 4.9 divide_multiply_fusion.42
  274.9 5.3 collective-permute-done.3
  284.4 23.9 %scatter_custom_fusion.2 = f32[27,12288]{0,1:T(8,128)} fusion(s32[8192]{0:T(1024)S(1)} %get-tuple-element.336, f32[8192,27]{1,0:T(8,128)} %copy.162, f32[]{:T(128)} %constant.101.clone.1), kind=kCustom, calls=%fused_computation.42 | custom fusion | bytes 1327616 | tf_op jit(solution)/shard_map/scatter | solution.py:131
  335.3 5.3 collective-permute-start.10
  355.6 16.9 %all-to-all-done.2 = f32[27,8,4,384]{3,1,0,2:T(8,128)} async-done(((f32[27,8,4,384]{3,1,0,2:T(8,128)}), f32[27,8,4,384]{3,1,0,2:T(8,128)}, u32[]{:S(2)}, u32[]{:S(2)}) %all-to-all-start.2) | async-done | bytes 1327136 | tf_op jit(solution)/shard_map/all_to_all | solution.py:134
  379.3 64.9 %while.45 = (s32[]{:T(128)}, f32[24,3,512]{2,1,0:T(4,128)S(1)}, s32[24,512]{1,0:T(8,128)S(1)}, f32[3,256,512]{1,2,0:T(8,128)S(1)}, f32[24,24,512]{2,1,0:T(8,128)}, /*index=5*/s32[]{:T(128)}, s32[]{:T(128)}, s32[]{}, s32[]{}) while((s32[]{:T(128)}, f32[24,3,512]{2,1,0:T(4,128)S(1)}, s32[24,512]{1,0:T(8,128)S(1)}, f32[3,256,512]{1,2,0:T(8,128)S(1)}, ...), condition=%wide.region_8.9_spmd, body=%wide.region_6.8_spmd.sunk | while | flops 2417916416 | bytes 4108425 | solution.py:174
  445.0 8.2 %all-to-all-start.3 = ((f32[3,8,4,384]{3,2,0,1:T(4,128)}), f32[3,8,4,384]{3,2,0,1:T(4,128)S(1)}, u32[]{:S(2)}, u32[]{:S(2)}) async-start(f32[3,8,4,384]{3,2,0,1:T(4,128)} %copy.176), calls=%async_computation.3 | async-start | bytes 294912 | tf_op jit(solution)/shard_map/all_to_all | solution.py:177
  454.3 6.4 %all-to-all-done.3 = f32[3,8,4,384]{3,2,0,1:T(4,128)S(1)} async-done(((f32[3,8,4,384]{3,2,0,1:T(4,128)}), f32[3,8,4,384]{3,2,0,1:T(4,128)S(1)}, u32[]{:S(2)}, u32[]{:S(2)}) %all-to-all-start.3) | async-done | bytes 147488 | tf_op jit(solution)/shard_map/all_to_all | solution.py:177
  464.9 85.0 %while.47 = (s32[]{:T(128)}, f32[3,256,512]{1,2,0:T(8,128)S(1)}, f32[24,3,512]{2,0,1:T(8,128)S(1)}, f32[24,24,512]{2,1,0:T(8,128)}, s32[24,512]{1,0:T(8,128)S(1)}, /*index=5*/s32[]{:T(128)}, s32[]{:T(128)}, s32[]{}, s32[]{}) while((s32[]{:T(128)}, f32[3,256,512]{1,2,0:T(8,128)S(1)}, f32[24,3,512]{2,0,1:T(8,128)S(1)}, ...), condition=%wide.region_10.11_spmd.clone, body=%wide.region_9.10_spmd.clone.sunk | while | flops 2417917952 | bytes 5689491 | solution.py:198
  555.4 30.5 %gather_fusion.3 = f32[8192,3]{1,0:T(8,128)} fusion(f32[3,12288]{0,1:T(8,128)} %bitcast.164, s32[8192]{0:T(1024)S(1)} %get-tuple-element.335), kind=kCustom, calls=%fused_computation.3 | custom fusion | bytes 229376 | tf_op jit(solution)/shard_map/jit(_take)/gather | solution.py:201
  (481 shorter events, 244.7 us)
Async XLA Ops:
  0.6 14.9 %copy-start = (s32[8192,1]{0,1:T(1,128)S(1)}, s32[8192,1]{0,1:T(1,128)}, u32[]{:S(2)}) copy-start(s32[8192,1]{0,1:T(1,128)} %param.17) | copy-start | bytes 98308
  1.4 269.2 %collective-permute-start.1 = (f32[4,1,256]{2,1,0:T(1,128)S(1)}, f32[4,1,256]{2,1,0:T(1,128)S(1)}, u32[]{:S(2)}, u32[]{:S(2)}) collective-permute-start(f32[4,1,256]{2,1,0:T(1,128)S(1)} %get-tuple-element.300), channel_id=1, source_target_pairs={{0,1},{1,2},{2,3},{3,4},{4,5},{5,6},{6,7},{7,8},{8,9},{9,10},{10,1... | collective-permute-start | bytes 12296 | tf_op jit(solution)/shard_map/ppermute | solution.py:42
  2.0 268.6 %collective-permute-start = (f32[4,1,256]{2,1,0:T(1,128)S(1)}, f32[4,1,256]{2,1,0:T(1,128)S(1)}, u32[]{:S(2)}, u32[]{:S(2)}) collective-permute-start(f32[4,1,256]{2,1,0:T(1,128)S(1)} %get-tuple-element.299), channel_id=1, source_target_pairs={{1,0},{2,1},{3,2},{4,3},{5,4},{6,5},{7,6},{8,7},{9,8},{10,9},{11,1... | collective-permute-start | bytes 12296 | tf_op jit(solution)/shard_map/ppermute | solution.py:44
  61.0 170.1 %copy-start.1 = (f32[3,32,256]{2,1,0:T(8,128)S(1)}, f32[3,32,256]{2,1,0:T(8,128)}, u32[]{:S(2)}) copy-start(f32[3,32,256]{2,1,0:T(8,128)} %param.14) | copy-start | bytes 294916
  71.6 159.8 %copy-start.6 = (f32[32,256]{1,0:T(8,128)S(1)}, f32[32,256]{1,0:T(8,128)}, u32[]{:S(2)}) copy-start(f32[32,256]{1,0:T(8,128)} %param.15) | copy-start | bytes 98308
  71.6 159.9 %copy-start.2 = (f32[3,8192]{1,0:T(4,128)S(1)}, f32[3,8192]{1,0:T(4,128)}, u32[]{:S(2)}) copy-start(f32[3,8192]{1,0:T(4,128)} %param.19) | copy-start | bytes 294916
  80.0 190.6 %copy-start.5 = (f32[32,256]{1,0:T(8,128)S(1)}, f32[32,256]{1,0:T(8,128)}, u32[]{:S(2)}) copy-start(f32[32,256]{1,0:T(8,128)} %param.16) | copy-start | bytes 98308
  157.8 172.5 %all-to-all-start = ((s32[1,8,4,384]{3,2,0,1:T(4,128)}), s32[1,8,4,384]{3,2,0,1:T(4,128)S(1)}, u32[]{:S(2)}, u32[]{:S(2)}) async-start(s32[1,8,4,384]{3,2,0,1:T(4,128)} %reshape.154), calls=%async_computation | async-start | bytes 98304 | tf_op jit(solution)/shard_map/all_to_all | solution.py:144
  270.9 4.0 collective-permute-start.2
  273.6 6.6 %collective-permute-start.3 = (f32[3,1,256]{2,1,0:T(1,128)S(1)}, f32[3,1,256]{2,1,0:T(1,128)S(1)}, u32[]{:S(2)}, u32[]{:S(2)}) collective-permute-start(f32[3,1,256]{2,1,0:T(1,128)S(1)} %get-tuple-element.330), channel_id=1, source_target_pairs={{0,1},{1,2},{2,3},{3,4},{4,5},{5,6},{6,7},{7,8},{8,9},{9,10},{10,1... | collective-permute-start | bytes 9224 | tf_op jit(solution)/shard_map/ppermute | solution.py:42
  316.6 17.7 %collective-permute-start.4 = (f32[27,1,4,384]{3,2,0,1:T(4,128)}, f32[27,1,4,384]{3,2,0,1:T(4,128)}, u32[]{:S(2)}, u32[]{:S(2)}) collective-permute-start(f32[27,1,4,384]{3,2,0,1:T(4,128)} %bitcast.183), channel_id=1, source_target_pairs={{0,4},{4,0},{8,12},{12,8},{16,20},{20,16},{24,28},{28,24},{1,5},{5... | collective-permute-start | bytes 497672 | tf_op jit(solution)/shard_map/ppermute | solution.py:30
  319.3 16.0 %collective-permute-start.5 = (f32[27,1,4,384]{3,2,0,1:T(4,128)}, f32[27,1,4,384]{3,2,0,1:T(4,128)}, u32[]{:S(2)}, u32[]{:S(2)}) collective-permute-start(f32[27,1,4,384]{3,2,0,1:T(4,128)} %bitcast.61), channel_id=1, source_target_pairs={{0,8},{4,12},{8,0},{12,4},{16,24},{20,28},{24,16},{28,20},{1,9},{5... | collective-permute-start | bytes 497672 | tf_op jit(solution)/shard_map/ppermute | solution.py:30
  321.4 20.2 %collective-permute-start.6 = (f32[27,1,4,384]{3,2,0,1:T(4,128)}, f32[27,1,4,384]{3,2,0,1:T(4,128)}, u32[]{:S(2)}, u32[]{:S(2)}) collective-permute-start(f32[27,1,4,384]{3,2,0,1:T(4,128)} %bitcast.63), channel_id=1, source_target_pairs={{0,12},{4,8},{8,4},{12,0},{16,28},{20,24},{24,20},{28,16},{1,13},{... | collective-permute-start | bytes 497672 | tf_op jit(solution)/shard_map/ppermute | solution.py:30
  325.8 16.7 %collective-permute-start.7 = (f32[27,1,4,384]{3,2,0,1:T(4,128)}, f32[27,1,4,384]{3,2,0,1:T(4,128)}, u32[]{:S(2)}, u32[]{:S(2)}) collective-permute-start(f32[27,1,4,384]{3,2,0,1:T(4,128)} %bitcast.65), channel_id=1, source_target_pairs={{0,16},{4,20},{8,24},{12,28},{16,0},{20,4},{24,8},{28,12},{1,17},{... | collective-permute-start | bytes 497672 | tf_op jit(solution)/shard_map/ppermute | solution.py:30
  326.7 7.6 %copy-start.3 = (f32[8,27,1,4,384]{4,3,1,0,2:T(4,128)S(1)}, f32[8,27,1,4,384]{4,3,1,0,2:T(4,128)}, u32[]{:S(2)}) copy-start(f32[8,27,1,4,384]{4,3,1,0,2:T(4,128)} %bitcast_dynamic-update-slice_fusion.8) | copy-start | bytes 3981316
  326.7 16.8 %collective-permute-start.8 = (f32[27,1,4,384]{3,2,0,1:T(4,128)}, f32[27,1,4,384]{3,2,0,1:T(4,128)S(1)}, u32[]{:S(2)}, u32[]{:S(2)}) collective-permute-start(f32[27,1,4,384]{3,2,0,1:T(4,128)} %bitcast.67), channel_id=1, source_target_pairs={{0,20},{4,16},{8,28},{12,24},{16,4},{20,0},{24,12},{28,8},{1,21},{... | collective-permute-start | bytes 497672 | tf_op jit(solution)/shard_map/ppermute | solution.py:30
  330.9 19.7 %all-to-all-start.1 = ((s32[1,8,4,384]{3,1,0,2:T(8,128)}), s32[1,8,4,384]{3,1,0,2:T(8,128)S(1)}, u32[]{:S(2)}, u32[]{:S(2)}) async-start(s32[1,8,4,384]{3,1,0,2:T(8,128)} %copy.160), calls=%async_computation.1 | async-start | bytes 98304 | tf_op jit(solution)/shard_map/all_to_all | solution.py:143
  334.2 9.3 %collective-permute-start.9 = (f32[27,1,4,384]{3,2,0,1:T(4,128)}, f32[27,1,4,384]{3,2,0,1:T(4,128)S(1)}, u32[]{:S(2)}, u32[]{:S(2)}) collective-permute-start(f32[27,1,4,384]{3,2,0,1:T(4,128)} %bitcast.182), channel_id=1, source_target_pairs={{0,24},{4,28},{8,16},{12,20},{16,8},{20,12},{24,0},{28,4},{1,25},{... | collective-permute-start | bytes 497672 | tf_op jit(solution)/shard_map/ppermute | solution.py:30
  335.3 12.7 %collective-permute-start.10 = (f32[27,1,4,384]{3,2,0,1:T(4,128)S(1)}, f32[27,1,4,384]{3,2,0,1:T(4,128)S(1)}, u32[]{:S(2)}, u32[]{:S(2)}) collective-permute-start(f32[27,1,4,384]{3,2,0,1:T(4,128)S(1)} %bitcast.181), channel_id=1, source_target_pairs={{0,28},{4,24},{8,20},{12,16},{16,12},{20,8},{24,4},{28,0},{1,29},{... | collective-permute-start | bytes 497672 | tf_op jit(solution)/shard_map/ppermute | solution.py:30
  350.6 4.4 copy-start.4
  350.6 21.9 %all-to-all-start.2 = ((f32[27,8,4,384]{3,1,0,2:T(8,128)}), f32[27,8,4,384]{3,1,0,2:T(8,128)}, u32[]{:S(2)}, u32[]{:S(2)}) async-start(f32[27,8,4,384]{3,1,0,2:T(8,128)} %copy.171), calls=%async_computation.2 | async-start | bytes 2654208 | tf_op jit(solution)/shard_map/all_to_all | solution.py:134
  376.3 3.0 copy-start.7
  445.0 15.6 %all-to-all-start.3 = ((f32[3,8,4,384]{3,2,0,1:T(4,128)}), f32[3,8,4,384]{3,2,0,1:T(4,128)S(1)}, u32[]{:S(2)}, u32[]{:S(2)}) async-start(f32[3,8,4,384]{3,2,0,1:T(4,128)} %copy.176), calls=%async_computation.3 | async-start | bytes 294912 | tf_op jit(solution)/shard_map/all_to_all | solution.py:177
  461.3 90.2 %all-to-all-start.4 = ((f32[3,8,4,384]{3,1,0,2:T(8,128)}), f32[3,8,4,384]{3,1,0,2:T(8,128)S(1)}, u32[]{:S(2)}, u32[]{:S(2)}) async-start(f32[3,8,4,384]{3,1,0,2:T(8,128)} %copy.177), calls=%async_computation.4 | async-start | bytes 294912 | tf_op jit(solution)/shard_map/all_to_all | solution.py:176
